TPU v7x, 32 devices: a whole 2x2x4 slice. The times are simulated.
32 devices in a mesh: gz: 16 (over z, y, x), ta: 2 (over core).
Axes of the slice: x: 2, y: 2, z: 4, core: 2. Of those that a mesh axis runs over, the one named last changes fastest.
Arguments:
- position: float32 [2, 48, 32, 512], P(None, 'gz', 'ta'), may hold values from -6 to 6
- gaps: float32 [2, 3, 48, 32, 512], P(None, None, 'gz', 'ta'), may hold values from -6 to 6
- weights: float32 [3, 48, 32, 512], P(None, 'gz', 'ta'), may hold values from 0.2 to 2
- deltas: int32 [3, 48, 32, 512], P(None, 'gz', 'ta'), may hold values from 0 to 8
- springs: int32 [2, 48, 32, 512], P(None, 'gz', 'ta'), may hold values 0 or 1
- damping: float32 [48, 32, 512], P('gz', 'ta'), may hold values from 0.1 to 1
- stiffness: float32 [2, 48], P(None, 'gz'), may hold values from 0.5 to 4
Outputs:
- update: float32 [2, 48, 32, 512], P(None, 'gz', 'ta')
- residual: float32 [2, 48, 32, 512], P(None, 'gz', 'ta')
All inputs are finite; a program needn't handle non-finite values. No bound on the sum of `springs` on one device may be relied on, other than what follows from the above.
Results may differ from a plain program's by a relative error of at most 0.00012.
Values sent between devices are 32-bit elements; how exact they have to be, the bound alone decides.
A program may use at most 64 MiB of HBM per device.

v0:
```python
import jax
import jax.numpy as jnp
from jax import lax
from jax.sharding import PartitionSpec as P

ITERS = 2


def passed_along(shard, axis, by):
    size = lax.axis_size(axis)
    pairs = [(i, i + by) for i in range(size) if 0 <= i + by < size]
    return lax.ppermute(shard, axis, pairs)


def extended_2(shard, sides, width):
    for axis, dim in sides:
        size, length = (lax.axis_size(axis), shard.shape[dim])
        up = [(i, (i + 1) % size) for i in range(size - 1)]
        down = [(j, i) for i, j in up]
        last = lax.slice_in_dim(shard, length - width, length, axis=dim)
        first = lax.slice_in_dim(shard, 0, width, axis=dim)
        before = lax.ppermute(last, axis, up)
        after = lax.ppermute(first, axis, down)
        shard = jnp.concatenate([before, shard, after], axis=dim)
    return shard


def shift_along(values, axis, step):
    if step == 0:
        return values
    length = values.shape[axis]
    widths = [(0, 0)] * values.ndim
    if step > 0:
        kept = lax.slice_in_dim(values, 0, length - step, axis=axis)
        widths[axis] = (step, 0)
    else:
        kept = lax.slice_in_dim(values, -step, length, axis=axis)
        widths[axis] = (0, -step)
    return jnp.pad(kept, widths)


def place_masks(delta):
    return [delta == place for place in range(9)]


def take_columns(field, masks):
    total = jnp.zeros_like(field)
    for place in range(9):
        total = total + jnp.where(masks[place], shift_along(field, 3, 4 - place), 0.0)
    return total


def put_columns(values, masks):
    total = jnp.zeros_like(values)
    for place in range(9):
        total = total + shift_along(jnp.where(masks[place], values, 0.0), 3, place - 4)
    return total


def column_valid(delta):
    columns_at = lax.broadcasted_iota(jnp.int32, delta.shape, 2)
    target = columns_at + delta - 4
    return jnp.where((target >= 0) & (target < delta.shape[2]), 1.0, 0.0).astype(jnp.float32)


def two_products(residual, image):
    return lax.psum((jnp.sum(residual * residual), jnp.sum(residual * image)), ("gz", "ta"))


def body(position, gaps, weights, deltas, springs, damping, stiffness):
    sec_count, row_count, col_count = damping.shape
    sections_at = lax.broadcasted_iota(jnp.int32, (sec_count, row_count, col_count), 0)
    rows_at = lax.broadcasted_iota(jnp.int32, (sec_count, row_count, col_count), 1)
    columns_at = lax.broadcasted_iota(jnp.int32, (sec_count, row_count, col_count), 2)
    first_section = lax.axis_index("gz") * sec_count
    all_sections = sec_count * lax.axis_size("gz")
    first_row = lax.axis_index("ta") * row_count
    all_rows = row_count * lax.axis_size("ta")
    along = stiffness[0][:, None, None]
    across = stiffness[1][:, None, None]
    horiz = jnp.where((springs[0] > 0) & (columns_at < col_count - 1), 1.0, 0.0).astype(jnp.float32)
    vert_own = jnp.where((springs[1] > 0) & (first_row + rows_at < all_rows - 1), 1.0, 0.0).astype(
        jnp.float32
    )
    above_mask = passed_along(springs[1][:, row_count - 1 :, :], "ta", 1)
    vert_ext = jnp.concatenate(
        [jnp.where(above_mask > 0, 1.0, 0.0).astype(jnp.float32), vert_own], axis=1
    )
    strength_own = []
    for slot in range(3):
        inside = jnp.where(first_section + sections_at + slot + 1 < all_sections, 1.0, 0.0).astype(
            jnp.float32
        )
        strength_own.append(weights[slot] * column_valid(deltas[slot]) * inside)
    strength_own = jnp.stack(strength_own, 0)

    def in_section(field):
        rimmed = extended_2(field, (("ta", 2),), 1)
        v_flux = across * vert_ext * (rimmed[:, :, 1:] - rimmed[:, :, :-1])
        h_flux = along * horiz * (shift_along(field, 3, -1) - field)
        return (
            damping * field
            - h_flux
            + shift_along(h_flux, 3, 1)
            + v_flux[:, :, :-1]
            - v_flux[:, :, 1:]
        )

    own_masks = [place_masks(deltas[slot]) for slot in range(3)]

    def coupled(field, gap_set):
        upper = passed_along(field, "gz", -1)
        extended = jnp.concatenate([field, upper], 1)
        forward = jnp.zeros_like(field)
        returned_sum = jnp.zeros_like(extended)
        for slot in range(3):
            offset = slot + 1
            partner = take_columns(extended[:, offset : offset + sec_count], own_masks[slot])
            mismatch = field - partner
            if gap_set is not None:
                mismatch = mismatch - gap_set[:, slot]
            pulled = strength_own[slot] * mismatch
            forward = forward + pulled
            returned_sum = returned_sum - shift_along(
                jnp.pad(put_columns(pulled, own_masks[slot]), ((0, 0), (0, 3), (0, 0), (0, 0))),
                1,
                offset,
            )
        incoming = passed_along(returned_sum[:, sec_count:], "gz", 1)
        own_part = returned_sum[:, :sec_count] + incoming
        return forward + own_part

    def operator(field, gap_set):
        return in_section(field) + coupled(field, gap_set)

    rhs = -operator(position, gaps)
    update = jnp.zeros_like(rhs)
    residual = rhs
    image = operator(residual, None)
    norm_now, product = two_products(residual, image)
    alpha = norm_now / product
    direction, moving = (residual, image)
    for step in range(ITERS):
        update = update + alpha * direction
        residual = residual - alpha * moving
        if step + 1 < ITERS:
            image = operator(residual, None)
            norm_next, product = two_products(residual, image)
            ratio = norm_next / norm_now
            alpha = norm_next / (product - ratio * norm_next / alpha)
            direction = residual + ratio * direction
            moving = image + ratio * moving
            norm_now = norm_next
    return (update, residual)


def solution(mesh):
    return jax.shard_map(
        body,
        mesh=mesh,
        in_specs=(
            P(None, "gz", "ta", None),
            P(None, None, "gz", "ta", None),
            P(None, "gz", "ta", None),
            P(None, "gz", "ta", None),
            P(None, "gz", "ta", None),
            P("gz", "ta", None),
            P(None, "gz"),
        ),
        out_specs=(P(None, "gz", "ta", None), P(None, "gz", "ta", None)),
        check_vma=False,
    )
```

profile of v0, /device:TPU:0, one launch (start us, length us, event | category | flops | bytes accessed | tf_op | source)
XLA Modules:
  0.0 175.5 jit_solution(5881419972991514225)
XLA Ops:
  0.6 1.4 collective-permute-start.3
  2.1 1.0 fusion.105
  3.0 1.3 collective-permute-start.1
  4.3 3.2 %collective-permute-start.2 = (f32[2,3,1,512]{3,2,1,0:T(1,128)S(1)}, f32[2,3,1,512]{3,2,1,0:T(1,128)S(1)}, u32[]{:S(2)}, u32[]{:S(2)}) collective-permute-start(f32[2,3,1,512]{3,2,1,0:T(1,128)S(1)} %get-tuple-element.166), channel_id=1, source_target_pairs={{0,1},{2,3},{4,5},{6,7},{8,9},{10,11},{12,13},{14,15},{16,17},{18,... | collective-permute-start | bytes 36872 | tf_op jit(solution)/shard_map/ppermute | solution.py:22
  7.5 0.9 slice_bitcast_fusion
  8.4 1.3 collective-permute-start
  9.9 0.2 compare_bitcast_fusion.26
  10.2 0.4 copy-done.6
  10.6 0.3 copy-done.4
  11.0 0.9 copy-done.5
  12.0 0.1 compare_bitcast_fusion.7
  13.4 0.2 fusion.99
  13.6 0.2 fusion.100
  13.8 0.2 fusion.101
  14.0 0.2 fusion.102
  14.2 0.9 copy-done.3
  15.1 0.4 fusion.84
  15.5 0.1 slice_select_fusion.63
  15.6 0.1 slice_select_fusion.62
  16.0 0.3 pad_add_fusion.7
  16.3 0.4 fusion.92
  17.3 0.3 pad_add_fusion.8
  18.1 0.4 fusion.93
  19.0 0.3 pad_add_fusion.6
  19.4 5.6 %collective-permute-start.4 = (f32[2,3,16,512]{3,2,1,0:T(8,128)S(1)}, f32[2,3,16,512]{3,2,1,0:T(8,128)S(1)}, u32[]{:S(2)}, u32[]{:S(2)}) collective-permute-start(f32[2,3,16,512]{3,2,1,0:T(8,128)S(1)} %slice.922), channel_id=1, source_target_pairs={{0,2},{2,4},{4,6},{6,8},{8,10},{10,12},{12,14},{14,16},{16,18},{18... | collective-permute-start | bytes 589832 | tf_op jit(solution)/shard_map/ppermute | solution.py:12
  25.2 3.6 %collective-permute-done.4 = f32[2,3,16,512]{3,2,1,0:T(8,128)S(1)} collective-permute-done((f32[2,3,16,512]{3,2,1,0:T(8,128)S(1)}, f32[2,3,16,512]{3,2,1,0:T(8,128)S(1)}, u32[]{:S(2)}, u32[]{:S(2)}) %collective-permute-start.4) | collective-permute-done | bytes 196640 | tf_op jit(solution)/shard_map/ppermute | solution.py:12
  28.8 0.2 fusion.97
  29.0 1.3 collective-permute-start.5
  30.3 3.0 %collective-permute-start.6 = (f32[2,3,1,512]{3,2,1,0:T(1,128)S(1)}, f32[2,3,1,512]{3,2,1,0:T(1,128)S(1)}, u32[]{:S(2)}, u32[]{:S(2)}) collective-permute-start(f32[2,3,1,512]{3,2,1,0:T(1,128)S(1)} %get-tuple-element.130), channel_id=1, source_target_pairs={{0,1},{2,3},{4,5},{6,7},{8,9},{10,11},{12,13},{14,15},{16,17},{18,... | collective-permute-start | bytes 36872 | tf_op jit(solution)/shard_map/ppermute | solution.py:22
  33.4 1.3 collective-permute-start.7
  34.8 7.9 %collective-permute-done.7 = f32[2,3,16,512]{3,2,1,0:T(8,128)S(1)} collective-permute-done((f32[2,3,16,512]{3,2,1,0:T(8,128)S(1)}, f32[2,3,16,512]{3,2,1,0:T(8,128)S(1)}, u32[]{:S(2)}, u32[]{:S(2)}) %collective-permute-start.7) | collective-permute-done | bytes 196640 | tf_op jit(solution)/shard_map/ppermute | solution.py:12
  42.6 0.2 fusion.37
  42.8 0.2 fusion.38
  43.1 0.2 fusion.39
  43.3 0.3 fusion.40
  43.6 0.4 subtract_multiply_fusion.2
  44.5 0.4 fusion.66
  45.4 0.4 fusion.49
  46.3 0.3 pad_add_fusion.4
  46.6 0.3 pad_add_fusion.5
  47.0 0.3 pad_add_fusion.3
  47.4 5.3 %collective-permute-start.8 = (f32[2,3,16,512]{3,2,1,0:T(8,128)S(1)}, f32[2,3,16,512]{3,2,1,0:T(8,128)S(1)}, u32[]{:S(2)}, u32[]{:S(2)}) collective-permute-start(f32[2,3,16,512]{3,2,1,0:T(8,128)S(1)} %slice.1020), channel_id=1, source_target_pairs={{0,2},{2,4},{4,6},{6,8},{8,10},{10,12},{12,14},{14,16},{16,18},{18... | collective-permute-start | bytes 589832 | tf_op jit(solution)/shard_map/ppermute | solution.py:12
  52.8 3.1 %collective-permute-done.8 = f32[2,3,16,512]{3,2,1,0:T(8,128)S(1)} collective-permute-done((f32[2,3,16,512]{3,2,1,0:T(8,128)S(1)}, f32[2,3,16,512]{3,2,1,0:T(8,128)S(1)}, u32[]{:S(2)}, u32[]{:S(2)}) %collective-permute-start.8) | collective-permute-done | bytes 196640 | tf_op jit(solution)/shard_map/ppermute | solution.py:12
  55.9 0.9 multiply_reduce_fusion.2
  56.8 44.6 %all-reduce.166 = (f32[]{:T(128)}, f32[]{:T(128)}) all-reduce(f32[]{:T(128)} %get-tuple-element.5, f32[]{:T(128)} %get-tuple-element.4), channel_id=1, replica_groups=mesh['gz'=16,'ta'=2] {'gz','ta'}, use_global_device_ids=true, to_apply=%region_1.2 | all-reduce | flops 2 | bytes 16 | tf_op jit(solution)/shard_map/psum | solution.py:67
  102.7 1.3 collective-permute-start.9
  104.0 3.0 %collective-permute-start.10 = (f32[2,3,1,512]{3,2,1,0:T(1,128)S(1)}, f32[2,3,1,512]{3,2,1,0:T(1,128)S(1)}, u32[]{:S(2)}, u32[]{:S(2)}) collective-permute-start(f32[2,3,1,512]{3,2,1,0:T(1,128)S(1)} %get-tuple-element.95), channel_id=1, source_target_pairs={{0,1},{2,3},{4,5},{6,7},{8,9},{10,11},{12,13},{14,15},{16,17},{18,... | collective-permute-start | bytes 36872 | tf_op jit(solution)/shard_map/ppermute | solution.py:22
  107.1 1.5 collective-permute-start.11
  108.6 7.1 %collective-permute-done.11 = f32[2,3,16,512]{3,2,1,0:T(8,128)S(1)} collective-permute-done((f32[2,3,16,512]{3,2,1,0:T(8,128)S(1)}, f32[2,3,16,512]{3,2,1,0:T(8,128)S(1)}, u32[]{:S(2)}, u32[]{:S(2)}) %collective-permute-start.11) | collective-permute-done | bytes 196640 | tf_op jit(solution)/shard_map/ppermute | solution.py:12
  115.7 0.2 fusion.4
  115.9 0.2 fusion.5
  116.1 0.2 fusion.6
  116.4 0.3 fusion.7
  116.7 0.4 subtract_multiply_fusion
  117.5 0.4 fusion.33
  118.5 0.4 fusion.16
  119.4 0.3 pad_add_fusion.1
  119.7 0.3 pad_add_fusion.2
  120.1 0.3 pad_add_fusion
  120.5 4.5 %collective-permute-start.12 = (f32[2,3,16,512]{3,2,1,0:T(8,128)S(1)}, f32[2,3,16,512]{3,2,1,0:T(8,128)S(1)}, u32[]{:S(2)}, u32[]{:S(2)}) collective-permute-start(f32[2,3,16,512]{3,2,1,0:T(8,128)S(1)} %slice.1118), channel_id=1, source_target_pairs={{0,2},{2,4},{4,6},{6,8},{8,10},{10,12},{12,14},{14,16},{16,18},{18... | collective-permute-start | bytes 589832 | tf_op jit(solution)/shard_map/ppermute | solution.py:12
  125.1 3.1 %collective-permute-done.12 = f32[2,3,16,512]{3,2,1,0:T(8,128)S(1)} collective-permute-done((f32[2,3,16,512]{3,2,1,0:T(8,128)S(1)}, f32[2,3,16,512]{3,2,1,0:T(8,128)S(1)}, u32[]{:S(2)}, u32[]{:S(2)}) %collective-permute-start.12) | collective-permute-done | bytes 196640 | tf_op jit(solution)/shard_map/ppermute | solution.py:12
  128.2 0.9 multiply_reduce_fusion
  129.1 41.0 %all-reduce.165 = (f32[]{:T(128)}, f32[]{:T(128)}) all-reduce(f32[]{:T(128)} %get-tuple-element.3, f32[]{:T(128)} %get-tuple-element.2), channel_id=1, replica_groups=mesh['gz'=16,'ta'=2] {'gz','ta'}, use_global_device_ids=true, to_apply=%region_5.6 | all-reduce | flops 2 | bytes 16 | tf_op jit(solution)/shard_map/psum | solution.py:67
  174.7 0.8 multiply_subtract_fusion
  (101 shorter events, 6.8 us)
Async XLA Ops:
  0.6 9.1 %copy-start = (f32[2,3,16,512]{3,2,1,0:T(8,128)S(1)}, f32[2,3,16,512]{3,2,1,0:T(8,128)}, u32[]{:S(2)}) copy-start(f32[2,3,16,512]{3,2,1,0:T(8,128)} %param.7) | copy-start | bytes 589828
  0.6 12.8 %collective-permute-start.3 = (f32[2,3,16,512]{3,2,1,0:T(8,128)}, f32[2,3,16,512]{3,2,1,0:T(8,128)S(1)}, u32[]{:S(2)}, u32[]{:S(2)}) collective-permute-start(f32[2,3,16,512]{3,2,1,0:T(8,128)} %param.7), channel_id=1, source_target_pairs={{2,0},{4,2},{6,4},{8,6},{10,8},{12,10},{14,12},{16,14},{18,16},{20... | collective-permute-start | bytes 589832 | tf_op jit(solution)/shard_map/ppermute | solution.py:12
  3.0 22.0 %collective-permute-start.1 = (f32[2,3,1,512]{3,2,1,0:T(1,128)S(1)}, f32[2,3,1,512]{3,2,1,0:T(1,128)S(1)}, u32[]{:S(2)}, u32[]{:S(2)}) collective-permute-start(f32[2,3,1,512]{3,2,1,0:T(1,128)S(1)} %get-tuple-element.167), channel_id=1, source_target_pairs={{1,0},{3,2},{5,4},{7,6},{9,8},{11,10},{13,12},{15,14},{17,16},{19,... | collective-permute-start | bytes 36872 | tf_op jit(solution)/shard_map/ppermute | solution.py:23
  4.3 5.6 %copy-start.1 = (s32[3,3,16,512]{3,2,1,0:T(8,128)S(1)}, s32[3,3,16,512]{3,2,1,0:T(8,128)}, u32[]{:S(2)}) copy-start(s32[3,3,16,512]{3,2,1,0:T(8,128)} %param.10) | copy-start | bytes 884740
  4.3 20.7 %collective-permute-start.2 = (f32[2,3,1,512]{3,2,1,0:T(1,128)S(1)}, f32[2,3,1,512]{3,2,1,0:T(1,128)S(1)}, u32[]{:S(2)}, u32[]{:S(2)}) collective-permute-start(f32[2,3,1,512]{3,2,1,0:T(1,128)S(1)} %get-tuple-element.166), channel_id=1, source_target_pairs={{0,1},{2,3},{4,5},{6,7},{8,9},{10,11},{12,13},{14,15},{16,17},{18,... | collective-permute-start | bytes 36872 | tf_op jit(solution)/shard_map/ppermute | solution.py:22
  8.4 4.9 %collective-permute-start = (s32[3,1,512]{2,1,0:T(1,128)S(1)}, s32[3,1,512]{2,1,0:T(1,128)S(1)}, u32[]{:S(2)}, u32[]{:S(2)}) collective-permute-start(s32[3,1,512]{2,1,0:T(1,128)S(1)} %slice.844), channel_id=1, source_target_pairs={{0,1},{2,3},{4,5},{6,7},{8,9},{10,11},{12,13},{14,15},{16,17},{18,... | collective-permute-start | bytes 18440 | tf_op jit(solution)/shard_map/ppermute | solution.py:12
  9.9 0.7 copy-start.6
  9.9 0.9 copy-start.4
  10.9 1.0 copy-start.5
  14.0 1.1 copy-start.3
  19.4 9.3 %copy-start.2 = (f32[3,16,512]{2,1,0:T(8,128)S(1)}, f32[3,16,512]{2,1,0:T(8,128)}, u32[]{:S(2)}) copy-start(f32[3,16,512]{2,1,0:T(8,128)} %param.12) | copy-start | bytes 294916
  19.4 9.3 %collective-permute-start.4 = (f32[2,3,16,512]{3,2,1,0:T(8,128)S(1)}, f32[2,3,16,512]{3,2,1,0:T(8,128)S(1)}, u32[]{:S(2)}, u32[]{:S(2)}) collective-permute-start(f32[2,3,16,512]{3,2,1,0:T(8,128)S(1)} %slice.922), channel_id=1, source_target_pairs={{0,2},{2,4},{4,6},{6,8},{8,10},{10,12},{12,14},{14,16},{16,18},{18... | collective-permute-start | bytes 589832 | tf_op jit(solution)/shard_map/ppermute | solution.py:12
  29.0 5.6 %collective-permute-start.5 = (f32[2,3,1,512]{3,2,1,0:T(1,128)S(1)}, f32[2,3,1,512]{3,2,1,0:T(1,128)S(1)}, u32[]{:S(2)}, u32[]{:S(2)}) collective-permute-start(f32[2,3,1,512]{3,2,1,0:T(1,128)S(1)} %get-tuple-element.131), channel_id=1, source_target_pairs={{1,0},{3,2},{5,4},{7,6},{9,8},{11,10},{13,12},{15,14},{17,16},{19,... | collective-permute-start | bytes 36872 | tf_op jit(solution)/shard_map/ppermute | solution.py:23
  30.3 4.3 %collective-permute-start.6 = (f32[2,3,1,512]{3,2,1,0:T(1,128)S(1)}, f32[2,3,1,512]{3,2,1,0:T(1,128)S(1)}, u32[]{:S(2)}, u32[]{:S(2)}) collective-permute-start(f32[2,3,1,512]{3,2,1,0:T(1,128)S(1)} %get-tuple-element.130), channel_id=1, source_target_pairs={{0,1},{2,3},{4,5},{6,7},{8,9},{10,11},{12,13},{14,15},{16,17},{18,... | collective-permute-start | bytes 36872 | tf_op jit(solution)/shard_map/ppermute | solution.py:22
  33.4 9.3 %collective-permute-start.7 = (f32[2,3,16,512]{3,2,1,0:T(8,128)S(1)}, f32[2,3,16,512]{3,2,1,0:T(8,128)S(1)}, u32[]{:S(2)}, u32[]{:S(2)}) collective-permute-start(f32[2,3,16,512]{3,2,1,0:T(8,128)S(1)} %get-tuple-element.12), channel_id=1, source_target_pairs={{2,0},{4,2},{6,4},{8,6},{10,8},{12,10},{14,12},{16,14},{18,16},{20... | collective-permute-start | bytes 589832 | tf_op jit(solution)/shard_map/ppermute | solution.py:12
  47.4 8.5 %collective-permute-start.8 = (f32[2,3,16,512]{3,2,1,0:T(8,128)S(1)}, f32[2,3,16,512]{3,2,1,0:T(8,128)S(1)}, u32[]{:S(2)}, u32[]{:S(2)}) collective-permute-start(f32[2,3,16,512]{3,2,1,0:T(8,128)S(1)} %slice.1020), channel_id=1, source_target_pairs={{0,2},{2,4},{4,6},{6,8},{8,10},{10,12},{12,14},{14,16},{16,18},{18... | collective-permute-start | bytes 589832 | tf_op jit(solution)/shard_map/ppermute | solution.py:12
  102.7 5.8 %collective-permute-start.9 = (f32[2,3,1,512]{3,2,1,0:T(1,128)S(1)}, f32[2,3,1,512]{3,2,1,0:T(1,128)S(1)}, u32[]{:S(2)}, u32[]{:S(2)}) collective-permute-start(f32[2,3,1,512]{3,2,1,0:T(1,128)S(1)} %get-tuple-element.96), channel_id=1, source_target_pairs={{1,0},{3,2},{5,4},{7,6},{9,8},{11,10},{13,12},{15,14},{17,16},{19,... | collective-permute-start | bytes 36872 | tf_op jit(solution)/shard_map/ppermute | solution.py:23
  104.0 4.5 %collective-permute-start.10 = (f32[2,3,1,512]{3,2,1,0:T(1,128)S(1)}, f32[2,3,1,512]{3,2,1,0:T(1,128)S(1)}, u32[]{:S(2)}, u32[]{:S(2)}) collective-permute-start(f32[2,3,1,512]{3,2,1,0:T(1,128)S(1)} %get-tuple-element.95), channel_id=1, source_target_pairs={{0,1},{2,3},{4,5},{6,7},{8,9},{10,11},{12,13},{14,15},{16,17},{18,... | collective-permute-start | bytes 36872 | tf_op jit(solution)/shard_map/ppermute | solution.py:22
  107.1 8.6 %collective-permute-start.11 = (f32[2,3,16,512]{3,2,1,0:T(8,128)S(1)}, f32[2,3,16,512]{3,2,1,0:T(8,128)S(1)}, u32[]{:S(2)}, u32[]{:S(2)}) collective-permute-start(f32[2,3,16,512]{3,2,1,0:T(8,128)S(1)} %multiply_subtract_fusion.1), channel_id=1, source_target_pairs={{2,0},{4,2},{6,4},{8,6},{10,8},{12,10},{14,12},{16,14},{18,16},{20... | collective-permute-start | bytes 589832 | tf_op jit(solution)/shard_map/ppermute | solution.py:12
  120.5 7.7 %collective-permute-start.12 = (f32[2,3,16,512]{3,2,1,0:T(8,128)S(1)}, f32[2,3,16,512]{3,2,1,0:T(8,128)S(1)}, u32[]{:S(2)}, u32[]{:S(2)}) collective-permute-start(f32[2,3,16,512]{3,2,1,0:T(8,128)S(1)} %slice.1118), channel_id=1, source_target_pairs={{0,2},{2,4},{4,6},{6,8},{8,10},{10,12},{12,14},{14,16},{16,18},{18... | collective-permute-start | bytes 589832 | tf_op jit(solution)/shard_map/ppermute | solution.py:12
where the time goes:
time: 176 us
  blocking collectives  85.6 us (49%)
  starting transfers between devices  34.1 us (19%)
  waiting for transfers between devices  24.8 us (14%)
  other arithmetic  16.8 us (10%)
  between operations  7.28 us (4%)
  local copies, waits for them, and re-layouts  6.93 us (4%)
    psum x2, blocking collectives, two_products(): lax.psum((jnp.sum(residual * residual), jnp.sum(residual * image)), ('gz'...  85.6 us
    ppermute x7, waiting for transfers between devices, passed_along(): return lax.ppermute(shard, axis, pairs)  24.8 us
    ppermute x7, starting transfers between devices, passed_along(): return lax.ppermute(shard, axis, pairs)  21 us
    ppermute x3, starting transfers between devices, extended_2(): before = lax.ppermute(last, axis, up)  9.21 us
    select_n x36, other arithmetic, put_columns(): jnp.where(masks[place], values, 0.0)  4.26 us
    ppermute x3, starting transfers between devices, extended_2(): after = lax.ppermute(first, axis, down)  3.88 us
    mul x10, other arithmetic, coupled(): pulled = strength_own[slot] * mismatch  3.86 us
  transfers between devices with their start and end apart: 13, of which 5 were waited for; matrix products, arithmetic and copies ran while one was open for 5% of the time, Pallas kernels for 0%

commit v1 on v0

v1 whole, which is shorter than its diff:
```python
import functools

import jax
import jax.numpy as jnp
from jax import lax
from jax.experimental import pallas as pl
from jax.experimental.pallas import tpu as pltpu
from jax.sharding import PartitionSpec as P

MESH = pl.DeviceIdType.MESH
PLACES = 9
HALF = 8
OPS = 3


def rolled(values, step):
    axis = values.ndim - 1
    return values if step == 0 else pltpu.roll(values, step % values.shape[axis], axis)


def kernel(
    n, pos_h, gaps_h, wei_h, del_h, spr_h, dam_h, stiff,
    upd, res,
    v, up, tsend, trecv, esend, erecv, sall, gath,
    gaps, wei, dlt, spr, dam, vc, hc, hl, diag, qbuf,
    load_sem, vs_sem, vr_sem, ts_sem, tr_sem, es_sem, er_sem, gs_sem, gr_sem,
):
    g = lax.axis_index("gz")
    t = lax.axis_index("ta")
    secs, rows, cols = dam_h.shape
    chunks = rows // HALF
    other = {"gz": g, "ta": 1 - t}
    lower = {"gz": g - 1, "ta": t}
    upper = {"gz": g + 1, "ta": t}
    has_lower = g > 0
    has_upper = g < n - 1
    base = HALF

    loads = [
        pltpu.make_async_copy(pos_h, v.at[0, :, :, pl.ds(base, rows)], load_sem.at[0]),
        pltpu.make_async_copy(del_h, dlt, load_sem.at[1]),
        pltpu.make_async_copy(wei_h, wei, load_sem.at[2]),
        pltpu.make_async_copy(gaps_h, gaps, load_sem.at[3]),
        pltpu.make_async_copy(spr_h, spr, load_sem.at[4]),
        pltpu.make_async_copy(dam_h, dam, load_sem.at[5]),
    ]
    for load in loads:
        load.start()

    barrier = pltpu.get_barrier_semaphore()
    pl.semaphore_signal(barrier, inc=1, device_id=other, device_id_type=MESH)
    for j in range(1, n):
        pl.semaphore_signal(
            barrier, inc=1, device_id={"gz": lax.rem(g + j, n), "ta": t}, device_id_type=MESH
        )

    @pl.when(jnp.logical_not(has_upper))
    def _():
        up[...] = jnp.zeros_like(up)

    @pl.when(jnp.logical_not(has_lower))
    def _():
        trecv[...] = jnp.zeros_like(trecv)

    esend[...] = jnp.zeros_like(esend)

    def rows_at(h):
        return pl.ds(h * HALF, HALF)

    def v_copy(op, h):
        return pltpu.make_async_remote_copy(
            v.at[op, :, :, pl.ds(base + h * HALF, HALF)], up.at[op, :, :, rows_at(h)],
            vs_sem.at[op, h], vr_sem.at[op, h], device_id=lower, device_id_type=MESH,
        )

    def comps(op):
        return 3 if op == 0 else 2

    def t_copy(op, h):
        part = pl.ds(0, comps(op))
        return pltpu.make_async_remote_copy(
            tsend.at[op, part, :, rows_at(h)], trecv.at[op, part, :, rows_at(h)],
            ts_sem.at[op, h], tr_sem.at[op, h], device_id=upper, device_id_type=MESH,
        )

    def e_copy(op):
        return pltpu.make_async_remote_copy(
            esend.at[op], erecv.at[op], es_sem.at[op], er_sem.at[op],
            device_id=other, device_id_type=MESH,
        )

    def send_edges(op):
        for comp in range(2):
            for z in range(secs):
                top = v[op, comp, z, base : base + 1, :]
                bottom = v[op, comp, z, base + rows - 1 : base + rows, :]
                k = comp * secs + z
                esend[op, k : k + 1, :] = jnp.where(t == 0, bottom, top)
        if op == 0:
            for z in range(secs):
                k = 2 * secs + z
                esend[op, k : k + 1, :] = jnp.where(
                    spr[1, z, rows - 1 : rows, :] > 0, 1.0, 0.0
                ).astype(jnp.float32)
        e_copy(op).start()

    def take_edges(op):
        e_copy(op).wait_recv()
        for comp in range(2):
            for z in range(secs):
                k = comp * secs + z
                row = erecv[op, k : k + 1, :]
                v[op, comp, z, base - 1 : base, :] = jnp.where(t == 1, row, 0.0)
                v[op, comp, z, base + rows : base + rows + 1, :] = jnp.where(t == 0, row, 0.0)
        if op == 0:
            for z in range(secs):
                k = 2 * secs + z
                row = stiff[1, z] * erecv[op, k : k + 1, :]
                vc[z, base - 1 : base, :] = jnp.where(t == 1, row, 0.0)

    def scatter(op, h, dest):
        sources = [(dest - k - 1, k) for k in range(3) if 0 <= dest - k - 1 < secs]
        terms = []
        for z, k in sources:
            w = wei[k, z, rows_at(h)]
            field = v[op, :, z, pl.ds(base + h * HALF, HALF)]
            if op == 0:
                field = field - gaps[:, k, z, rows_at(h)]
                u = jnp.concatenate([w[None] * field, w[None]], 0)
            else:
                u = w[None] * field
            terms.append((dlt[k, z, rows_at(h)], u))
        total = None
        for place in range(PLACES):
            part = None
            for d, u in terms:
                one = jnp.where((d == place)[None], u, 0.0)
                part = one if part is None else part + one
            part = rolled(part, place - 4)
            total = part if total is None else total + part
        return total

    def send_up(op, h):
        for d in range(secs):
            tsend[op, pl.ds(0, comps(op)), d, rows_at(h)] = scatter(op, h, secs + d)

        @pl.when(has_upper)
        def _():
            t_copy(op, h).start()

    def send_down(op, h):
        @pl.when(has_lower)
        def _():
            v_copy(op, h).start()

    loads[0].wait()
    pl.semaphore_wait(barrier, n)
    for h in range(chunks):
        send_down(0, h)

    loads[1].wait()
    loads[2].wait()
    shape = (HALF, cols)
    columns_at = lax.broadcasted_iota(jnp.int32, shape, 1)
    row_at = lax.broadcasted_iota(jnp.int32, shape, 0)
    for k in range(3):
        for z in range(secs):
            inside = jnp.where(g * secs + z + k + 1 < n * secs, 1.0, 0.0).astype(jnp.float32)
            for h in range(chunks):
                target = columns_at + dlt[k, z, rows_at(h)] - 4
                valid = (target >= 0) & (target < cols)
                wei[k, z, rows_at(h)] = jnp.where(valid, wei[k, z, rows_at(h)], 0.0) * inside
    loads[3].wait()
    for h in range(chunks):
        send_up(0, h)
    loads[4].wait()
    send_edges(0)
    loads[5].wait()
    vc[...] = jnp.zeros_like(vc)
    for z in range(secs):
        for h in range(chunks):
            last = jnp.where((t == 1) & (row_at == HALF - 1), 0.0, 1.0) if h == chunks - 1 else 1.0
            vc[z, pl.ds(base + h * HALF, HALF)] = (
                stiff[1, z] * jnp.where(spr[1, z, rows_at(h)] > 0, 1.0, 0.0).astype(jnp.float32) * last
            )
            right = stiff[0, z] * jnp.where(
                (spr[0, z, rows_at(h)] > 0) & (columns_at < cols - 1), 1.0, 0.0
            ).astype(jnp.float32)
            hc[z, rows_at(h)] = right
            left = rolled(right, 1)
            hl[z, rows_at(h)] = left
            total = dam[z, rows_at(h)] + right + left
            for k in range(3):
                total = total + wei[k, z, rows_at(h)]
            diag[z, rows_at(h)] = total

    def local(op, h, write):
        here = pl.ds(base + h * HALF, HALF)
        own = {}
        for d in range(1, secs):
            own[d] = scatter(op, h, d)
            if op == 0:
                diag[d, rows_at(h)] = diag[d, rows_at(h)] + own[d][2]
        acc = [None] * secs
        for z in range(secs):
            center = v[op, :, z, here]
            acc[z] = -(
                hc[z, rows_at(h)][None] * rolled(center, -1)
                + hl[z, rows_at(h)][None] * rolled(center, 1)
            )
            if z > 0:
                acc[z] = acc[z] - own[z][0:2]
            if op == 0:
                for k in range(3):
                    acc[z] = acc[z] - wei[k, z, rows_at(h)][None] * gaps[:, k, z, rows_at(h)]

        def gather(s):
            field = v[op, :, s, here] if s < secs else up[op, :, s - secs, rows_at(h)]
            sources = [(s - k - 1, k) for k in range(3) if 0 <= s - k - 1 < secs]
            got = [None] * len(sources)
            for place in range(PLACES):
                moved = rolled(field, 4 - place)
                for i, (z, k) in enumerate(sources):
                    if got[i] is None:
                        got[i] = moved
                    else:
                        got[i] = jnp.where((dlt[k, z, rows_at(h)] == place)[None], moved, got[i])
            for i, (z, k) in enumerate(sources):
                acc[z] = acc[z] - wei[k, z, rows_at(h)][None] * got[i]

        for s in range(1, secs):
            gather(s)
        if h == 0:
            take_edges(op)
        for z in range(secs):
            if op == 0:
                above = vc[z, base + h * HALF - 1 : base + h * HALF - 1 + HALF, :]
                diag[z, rows_at(h)] = diag[z, rows_at(h)] + vc[z, here] + above
            first = base + h * HALF
            acc[z] = acc[z] - (
                vc[z, here][None] * v[op, :, z, first + 1 : first + 1 + HALF, :]
                + vc[z, first - 1 : first - 1 + HALF, :][None]
                * v[op, :, z, first - 1 : first - 1 + HALF, :]
            )

        @pl.when(has_lower)
        def _():
            t_copy(op, h).wait_recv()

        @pl.when(has_upper)
        def _():
            v_copy(op, h).wait_recv()

        for s in range(secs, 2 * secs):
            gather(s)
        for z in range(secs):
            if op == 0:
                diag[z, rows_at(h)] = diag[z, rows_at(h)] + trecv[op, 2, z, rows_at(h)]
            image = (
                acc[z]
                + diag[z, rows_at(h)][None] * v[op, :, z, here]
                - trecv[op, 0:2, z, rows_at(h)]
            )
            write(z, image)

    dots = [jnp.zeros(shape, jnp.float32) for _ in range(4)]

    def dot_into(i, a, b):
        dots[i] = dots[i] + a[0] * b[0] + a[1] * b[1]

    for op in range(OPS):
        for h in range(chunks):
            here = pl.ds(base + h * HALF, HALF)

            def write(z, image, op=op, h=h, here=here):
                if op == 0:
                    v[1, :, z, here] = -image
                    dot_into(0, image, image)
                elif op == 1:
                    v[2, :, z, here] = image
                    dot_into(1, v[1, :, z, here], image)
                    dot_into(2, image, image)
                else:
                    qbuf[:, z, rows_at(h)] = image
                    dot_into(3, v[2, :, z, here], image)

            local(op, h, write)
            if op + 1 < OPS:
                send_down(op + 1, h)
                send_up(op + 1, h)
        if op + 1 < OPS:
            send_edges(op + 1)

    lanes = 128
    packed = jnp.zeros((8, lanes), jnp.float32)
    sub = lax.broadcasted_iota(jnp.int32, (8, lanes), 0)
    for i in range(4):
        row = jnp.sum(dots[i], axis=0, keepdims=True)
        part = row[:, 0:lanes]
        for c in range(lanes, cols, lanes):
            part = part + row[:, c : c + lanes]
        packed = jnp.where(sub == i, part, packed)
    esend[OPS, 0:8, 0:lanes] = packed
    e_copy(OPS).start()
    e_copy(OPS).wait_recv()
    packed = packed + erecv[OPS, 0:8, 0:lanes]
    sall[...] = packed
    pushes = []
    for j in range(1, n):
        pushes.append(
            pltpu.make_async_remote_copy(
                sall, gath.at[j - 1], gs_sem.at[j - 1], gr_sem.at[j - 1],
                device_id={"gz": lax.rem(g + j, n), "ta": t}, device_id_type=MESH,
            )
        )
    for push in pushes:
        push.start()
    for push in pushes:
        push.wait_recv()
    total = packed
    for j in range(1, n):
        total = total + gath[j - 1]
    total = jnp.sum(total, axis=1, keepdims=True)
    rr, rm, mm, mq = (total[i : i + 1, :] for i in range(4))
    alpha0 = rr / rm
    rr1 = alpha0 * (alpha0 * mm) - rr
    ratio = rr1 / rr
    one = 1.0 + ratio
    curve = one * one * rm - 2.0 * one * alpha0 * mm + alpha0 * alpha0 * mq
    alpha1 = rr1 / curve
    for z in range(secs):
        for h in range(chunks):
            here = pl.ds(base + h * HALF, HALF)
            for comp in range(2):
                r0 = v[1, comp, z, here]
                m0 = v[2, comp, z, here]
                q = qbuf[comp, z, rows_at(h)]
                r1 = r0 - alpha0 * m0
                upd[comp, z, rows_at(h)] = alpha0 * r0 + alpha1 * (r1 + ratio * r0)
                res[comp, z, rows_at(h)] = r1 - alpha1 * (one * m0 - alpha0 * q)

    for push in pushes:
        push.wait_send()
    for op in range(OPS + 1):
        e_copy(op).wait_send()

    @pl.when(has_lower)
    def _():
        for op in range(OPS):
            for h in range(chunks):
                v_copy(op, h).wait_send()

    @pl.when(has_upper)
    def _():
        for op in range(OPS):
            for h in range(chunks):
                t_copy(op, h).wait_send()


def body(position, gaps, weights, deltas, springs, damping, stiffness):
    secs, rows, cols = damping.shape
    n = lax.axis_size("gz")
    chunks = rows // HALF
    f32, i32 = jnp.float32, jnp.int32
    edge = -(-3 * secs // 8) * 8
    padded = rows + 2 * HALF
    dma = pltpu.SemaphoreType.DMA
    out = jax.ShapeDtypeStruct(position.shape, f32)
    anyspace = pl.BlockSpec(memory_space=pl.ANY)
    vmem = pl.BlockSpec(memory_space=pltpu.VMEM)
    return pl.pallas_call(
        functools.partial(kernel, n),
        out_shape=(out, out),
        in_specs=[anyspace] * 6 + [pl.BlockSpec(memory_space=pltpu.SMEM)],
        out_specs=(vmem, vmem),
        scratch_shapes=[
            pltpu.VMEM((OPS, 2, secs, padded, cols), f32),
            pltpu.VMEM((OPS, 2, secs, rows, cols), f32),
            pltpu.VMEM((OPS, 3, secs, rows, cols), f32),
            pltpu.VMEM((OPS, 3, secs, rows, cols), f32),
            pltpu.VMEM((OPS + 1, edge, cols), f32),
            pltpu.VMEM((OPS + 1, edge, cols), f32),
            pltpu.VMEM((8, 128), f32),
            pltpu.VMEM((n - 1, 8, 128), f32),
            pltpu.VMEM(gaps.shape, f32),
            pltpu.VMEM(weights.shape, f32),
            pltpu.VMEM(deltas.shape, i32),
            pltpu.VMEM(springs.shape, i32),
            pltpu.VMEM(damping.shape, f32),
            pltpu.VMEM((secs, padded, cols), f32),
            pltpu.VMEM(damping.shape, f32),
            pltpu.VMEM(damping.shape, f32),
            pltpu.VMEM(damping.shape, f32),
            pltpu.VMEM(position.shape, f32),
            dma((6,)),
            dma((OPS, chunks)), dma((OPS, chunks)),
            dma((OPS, chunks)), dma((OPS, chunks)),
            dma((OPS + 1,)), dma((OPS + 1,)),
            dma((n - 1,)), dma((n - 1,)),
        ],
        compiler_params=pltpu.CompilerParams(
            collective_id=0, has_side_effects=True, vmem_limit_bytes=48 * 2**20
        ),
    )(position, gaps, weights, deltas, springs, damping, stiffness)


def solution(mesh):
    return jax.shard_map(
        body,
        mesh=mesh,
        in_specs=(
            P(None, "gz", "ta", None),
            P(None, None, "gz", "ta", None),
            P(None, "gz", "ta", None),
            P(None, "gz", "ta", None),
            P(None, "gz", "ta", None),
            P("gz", "ta", None),
            P(None, "gz"),
        ),
        out_specs=(P(None, "gz", "ta", None), P(None, "gz", "ta", None)),
        check_vma=False,
    )
```

time: 176 us -> 53.6 us (0.30)
  blocking collectives: 85.6 us -> 0 us
  Pallas kernels: 0 us -> 44.9 us
  starting transfers between devices: 34.1 us -> 0 us
  waiting for transfers between devices: 24.8 us -> 0 us
  other arithmetic: 16.8 us -> 0 us
  between operations: 7.28 us -> 0.66 us
    psum x2 -> x0, blocking collectives: 85.6 us -> none  [two_products(): lax.psum((jnp.sum(residual * residual), jnp.sum(residual * image)), ('gz'...]
    pallas_call x0 -> x1, Pallas kernels: none -> 44.9 us  [body(): pl.pallas_call(functools.partial(kernel, n), out_shape=(out, out), in_spe...]
    ppermute x13 -> x0, starting transfers between devices: 34.1 us -> none  [the longest x7 21 us: passed_along(): return lax.ppermute(shard, axis, pairs)]
    ppermute x13 -> x0, waiting for transfers between devices: 24.8 us -> none  [the longest x7 24.8 us: passed_along(): return lax.ppermute(shard, axis, pairs)]
    unnamed x14 -> x16, local copies, waits for them, and re-layouts: 2.48 us -> 7.76 us
    mul x18 -> x0, other arithmetic: 4.33 us -> none  [the longest x10 3.86 us: coupled(): pulled = strength_own[slot] * mismatch]
    select_n x39 -> x0, other arithmetic: 4.29 us -> none  [the longest x36 4.26 us: put_columns(): jnp.where(masks[place], values, 0.0)]
    slice x34 -> x0, local copies, waits for them, and re-layouts: 3.53 us -> none  [the longest x14 1.29 us: shift_along(): kept = lax.slice_in_dim(values, 0, length - step, axis=axis)]
  transfers between devices with their start and end apart: 13 -> 0, of which waited for: 5 -> 0; matrix products, arithmetic and copies ran while one was open for 5% -> 0% of each run, Pallas kernels for 0% -> 0%
where the time goes in v1:
time: 53.6 us; the launch traced here: 53.3 us
  Pallas kernels  44.9 us (84%)
  local copies, waits for them, and re-layouts  7.76 us (14%)
  between operations  0.66 us (1%)
    pallas_call x1, Pallas kernels, body(): pl.pallas_call(functools.partial(kernel, n), out_shape=(out, out), in_spe...  44.9 us
    unnamed x16, local copies, waits for them, and re-layouts  7.76 us

profile of v1, /device:TPU:0, one launch (start us, length us, event | category | flops | bytes accessed | tf_op | source)
XLA Modules:
  0.0 53.3 jit_solution(7550272810689246590)
XLA Ops:
  0.6 0.0 copy-start
  0.6 1.1 %copy-done = f32[2,3,3,16,512]{4,3,2,1,0:T(8,128)S(1)} copy-done((f32[2,3,3,16,512]{4,3,2,1,0:T(8,128)S(1)}, f32[2,3,3,16,512]{4,3,2,1,0:T(8,128)}, u32[]{:S(2)}) %copy-start) | copy-done | bytes 589848
  1.7 0.0 copy-start.1
  1.7 1.0 %copy-done.1 = f32[3,3,16,512]{3,2,1,0:T(8,128)S(1)} copy-done((f32[3,3,16,512]{3,2,1,0:T(8,128)S(1)}, f32[3,3,16,512]{3,2,1,0:T(8,128)}, u32[]{:S(2)}) %copy-start.1) | copy-done | bytes 294936
  2.7 0.0 copy-start.2
  2.7 1.0 %copy-done.2 = s32[3,3,16,512]{3,2,1,0:T(8,128)S(1)} copy-done((s32[3,3,16,512]{3,2,1,0:T(8,128)S(1)}, s32[3,3,16,512]{3,2,1,0:T(8,128)}, u32[]{:S(2)}) %copy-start.2) | copy-done | bytes 294936
  3.6 0.0 copy-start.3
  3.6 0.9 %copy-done.3 = f32[2,3,16,512]{3,2,1,0:T(8,128)S(1)} copy-done((f32[2,3,16,512]{3,2,1,0:T(8,128)S(1)}, f32[2,3,16,512]{3,2,1,0:T(8,128)}, u32[]{:S(2)}) %copy-start.3) | copy-done | bytes 196632
  4.5 0.0 copy-start.4
  4.6 0.9 %copy-done.4 = s32[2,3,16,512]{3,2,1,0:T(8,128)S(1)} copy-done((s32[2,3,16,512]{3,2,1,0:T(8,128)S(1)}, s32[2,3,16,512]{3,2,1,0:T(8,128)}, u32[]{:S(2)}) %copy-start.4) | copy-done | bytes 196632
  5.5 0.0 copy-start.5
  5.5 0.9 %copy-done.5 = f32[3,16,512]{2,1,0:T(8,128)S(1)} copy-done((f32[3,16,512]{2,1,0:T(8,128)S(1)}, f32[3,16,512]{2,1,0:T(8,128)}, u32[]{:S(2)}) %copy-start.5) | copy-done | bytes 98328
  6.4 0.0 copy-start.6
  6.4 0.7 %copy-done.6 = f32[2,3]{1,0:T(2,128)S(1)} copy-done((f32[2,3]{1,0:T(2,128)S(1)}, f32[2,3]{1,0:T(2,128)}, u32[]{:S(2)}) %copy-start.6) | copy-done | bytes 48
  7.0 44.9 %shard_map.86 = (f32[2,3,16,512]{3,2,1,0:T(8,128)S(1)}, f32[2,3,16,512]{3,2,1,0:T(8,128)S(1)}) custom-call(f32[2,3,16,512]{3,2,1,0:T(8,128)S(1)} %copy-done.3, f32[2,3,3,16,512]{4,3,2,1,0:T(8,128)S(1)} %copy-done, f32[3,3,16,512]{3,2,1,0:T(8,128)S(1)} %copy-done.1, s32[3,3,16,512]{3,2,1,0:T(8,128)S(1)} %copy-done.2, s32[2,3,16,512]{3,2,1,0:T(8,128)S(1)} %copy-done.4, ...), custom_call_target="tpu_custom_call" | custom-call | tf_op jit(solution)/shard_map/pallas_call | solution.py:371
  51.9 0.7 %copy.11 = f32[2,3,16,512]{3,2,1,0:T(8,128)} copy(f32[2,3,16,512]{3,2,1,0:T(8,128)S(1)} %get-tuple-element.4) | data formatting | bytes 393216
  52.6 0.7 %copy.12 = f32[2,3,16,512]{3,2,1,0:T(8,128)} copy(f32[2,3,16,512]{3,2,1,0:T(8,128)S(1)} %get-tuple-element.5) | data formatting | bytes 393216
Async XLA Ops:
  0.6 1.1 %copy-start = (f32[2,3,3,16,512]{4,3,2,1,0:T(8,128)S(1)}, f32[2,3,3,16,512]{4,3,2,1,0:T(8,128)}, u32[]{:S(2)}) copy-start(f32[2,3,3,16,512]{4,3,2,1,0:T(8,128)} %gaps_h.1) | copy-start | bytes 1769476
  1.7 1.0 %copy-start.1 = (f32[3,3,16,512]{3,2,1,0:T(8,128)S(1)}, f32[3,3,16,512]{3,2,1,0:T(8,128)}, u32[]{:S(2)}) copy-start(f32[3,3,16,512]{3,2,1,0:T(8,128)} %wei_h.1) | copy-start | bytes 884740
  2.7 1.0 %copy-start.2 = (s32[3,3,16,512]{3,2,1,0:T(8,128)S(1)}, s32[3,3,16,512]{3,2,1,0:T(8,128)}, u32[]{:S(2)}) copy-start(s32[3,3,16,512]{3,2,1,0:T(8,128)} %del_h.1) | copy-start | bytes 884740
  3.6 0.9 %copy-start.3 = (f32[2,3,16,512]{3,2,1,0:T(8,128)S(1)}, f32[2,3,16,512]{3,2,1,0:T(8,128)}, u32[]{:S(2)}) copy-start(f32[2,3,16,512]{3,2,1,0:T(8,128)} %pos_h.1) | copy-start | bytes 589828
  4.5 0.9 %copy-start.4 = (s32[2,3,16,512]{3,2,1,0:T(8,128)S(1)}, s32[2,3,16,512]{3,2,1,0:T(8,128)}, u32[]{:S(2)}) copy-start(s32[2,3,16,512]{3,2,1,0:T(8,128)} %spr_h.1) | copy-start | bytes 589828
  5.5 0.9 %copy-start.5 = (f32[3,16,512]{2,1,0:T(8,128)S(1)}, f32[3,16,512]{2,1,0:T(8,128)}, u32[]{:S(2)}) copy-start(f32[3,16,512]{2,1,0:T(8,128)} %dam_h.1) | copy-start | bytes 294916
  6.4 0.7 %copy-start.6 = (f32[2,3]{1,0:T(2,128)S(1)}, f32[2,3]{1,0:T(2,128)}, u32[]{:S(2)}) copy-start(f32[2,3]{1,0:T(2,128)} %stiff.1) | copy-start | bytes 76

commit v2 on v1

--- a/solution.py
+++ b/solution.py
@@ -155,8 +155,7 @@
 
     loads[0].wait()
     pl.semaphore_wait(barrier, n)
-    for h in range(chunks):
-        send_down(0, h)
+    send_down(0, 0)
 
     loads[1].wait()
     loads[2].wait()
@@ -173,6 +172,8 @@
     loads[3].wait()
     for h in range(chunks):
         send_up(0, h)
+        if h + 1 < chunks:
+            send_down(0, h + 1)
     loads[4].wait()
     send_edges(0)
     loads[5].wait()
@@ -399,7 +400,7 @@
             dma((n - 1,)), dma((n - 1,)),
         ],
         compiler_params=pltpu.CompilerParams(
-            collective_id=0, has_side_effects=True, vmem_limit_bytes=48 * 2**20
+            collective_id=0, has_side_effects=True, vmem_limit_bytes=67043328
         ),
     )(position, gaps, weights, deltas, springs, damping, stiffness)
 

time: 53.6 us -> 48.1 us (0.90)
  local copies, waits for them, and re-layouts: 7.76 us -> 2.34 us
    unnamed x16 -> x4, local copies, waits for them, and re-layouts: 7.76 us -> 2.34 us
where the time goes in v2:
time: 48.1 us; the launch traced here: 47.9 us
  Pallas kernels  44.9 us (93%)
  local copies, waits for them, and re-layouts  2.34 us (5%)
  between operations  0.65 us (1%)
    pallas_call x1, Pallas kernels, body(): pl.pallas_call(functools.partial(kernel, n), out_shape=(out, out), in_spe...  44.9 us
    unnamed x4, local copies, waits for them, and re-layouts  2.34 us

profile of v2, /device:TPU:0, one launch (start us, length us, event | category | flops | bytes accessed | tf_op | source)
XLA Modules:
  0.0 47.9 jit_solution(3278341376162970591)
XLA Ops:
  0.6 44.9 %shard_map.86 = (f32[2,3,16,512]{3,2,1,0:T(8,128)}, f32[2,3,16,512]{3,2,1,0:T(8,128)}) custom-call(f32[2,3,16,512]{3,2,1,0:T(8,128)} %pos_h.1, f32[2,3,3,16,512]{4,3,2,1,0:T(8,128)} %gaps_h.1, f32[3,3,16,512]{3,2,1,0:T(8,128)} %wei_h.1, s32[3,3,16,512]{3,2,1,0:T(8,128)} %del_h.1, s32[2,3,16,512]{3,2,1,0:T(8,128)} %spr_h.1, f32[3,16,512]{2,1,0:T(8,128)} %dam_h.1, ...), custom_call_target="tpu_custom_call" | custom-call | tf_op jit(solution)/shard_map/pallas_call | solution.py:372
  45.6 0.0 copy-start
  45.6 1.7 %copy.11 = f32[2,3,16,512]{3,2,1,0:T(8,128)} copy(f32[2,3,16,512]{3,2,1,0:T(8,128)} %get-tuple-element.4) | data formatting | bytes 393216
  47.2 0.0 copy-done
  47.3 0.7 %copy.12 = f32[2,3,16,512]{3,2,1,0:T(8,128)} copy(f32[2,3,16,512]{3,2,1,0:T(8,128)S(1)} %copy-done) | data formatting | bytes 393216
Async XLA Ops:
  45.6 1.7 %copy-start = (f32[2,3,16,512]{3,2,1,0:T(8,128)S(1)}, f32[2,3,16,512]{3,2,1,0:T(8,128)}, u32[]{:S(2)}) copy-start(f32[2,3,16,512]{3,2,1,0:T(8,128)} %get-tuple-element.5) | copy-start | bytes 589828
